TPU v7x, 32 devices: a whole 2x2x4 slice. The times are simulated.
32 devices in a mesh: gx: 8 (over y, x, core), gy: 4 (over z).
Axes of the slice: x: 2, y: 2, z: 4, core: 2. Of those that a mesh axis runs over, the one named last changes fastest.
Arguments:
- velocity: float32 [2, 320, 1024], P(None, 'gy', 'gx'), may hold values from -4 to 4
- stress: float32 [3, 320, 1024], P(None, 'gy', 'gx'), may hold values from -6 to 6
- wind: float32 [2, 320, 1024], P(None, 'gy', 'gx'), may hold values from -4 to 4
- strength: float32 [320, 1024], P('gy', 'gx'), may hold values from 0.5 to 2
- mass: float32 [320, 1024], P('gy', 'gx'), may hold values from 0.5 to 2
- land_mask: int32 [320, 1024], P('gy', 'gx'), may hold values 0 or 1
- region_mask: int32 [320, 1024], P('gy', 'gx'), may hold values 0 or 1
- observed: float32 [2, 320, 1024], P(None, 'gy', 'gx'), may hold values from -4 to 4
- start_index: int32 [1], replicated, may hold values from 0 to 112
Outputs:
- state_adjoint: float32 [5, 320, 1024], P(None, 'gy', 'gx')
- wind_direction: float32 [2, 320, 1024], P(None, 'gy', 'gx')
All inputs are finite; a program needn't handle non-finite values. No bound on the sum of `land_mask` or of `region_mask` on one device may be relied on, other than what follows from the above.
Results may differ from a plain program's by a relative error of at most 0.00002.
Values sent between devices are 32-bit elements; how exact they have to be, the bound alone decides.
A program may use at most 64 MiB of HBM per device.

v0:
```python
import jax
import jax.numpy as jnp
from jax import lax
from jax.sharding import PartitionSpec as P

STEPS = 8
SUBTOTAL = 120


ellipse_sq = 4.0
delta_floor = 0.04
time_step = 0.5
drag_rate = 1.0
norm_eps = 1e-06


def with_halo(block, sides, width, periodic):
    for axis, dim in sides:
        count = lax.axis_size(axis)
        forward = [(i, i + 1) for i in range(count - 1)]
        if periodic:
            forward.append((count - 1, 0))
        backward = [(target, source) for source, target in forward]
        low = lax.ppermute(
            lax.slice_in_dim(block, block.shape[dim] - width, None, axis=dim), axis, forward
        )
        high = lax.ppermute(lax.slice_in_dim(block, 0, width, axis=dim), axis, backward)
        block = jnp.concatenate([low, block, high], axis=dim)
    return block


def lat_halo(field):
    return with_halo(field, (("gy", 1),), 1, False)


def lon_halo(field):
    return with_halo(field, (("gx", 2),), 1, True)


def mirror(row):
    whole = lax.all_gather(row, "gx", axis=1, tiled=True)
    width = row.shape[1]
    partner = lax.axis_size("gx") - 1 - lax.axis_index("gx")
    return lax.dynamic_slice_in_dim(whole, partner * width, width, 1)


def top_flag():
    return lax.axis_index("gy") == lax.axis_size("gy") - 1


def extend(field, signs):
    rows = lat_halo(field)
    partner_row = mirror(field[:, -1, :])
    north = signs[:, None] * partner_row[:, ::-1]
    north = jnp.where(top_flag(), north, rows[:, -1, :])
    rows = rows.at[:, -1, :].set(north)
    return lon_halo(rows)


def retract(padded_bar, signs):
    inner = padded_bar[:, :, 1:-1]
    side_rims = jnp.stack([padded_bar[:, :, 0], padded_bar[:, :, -1]], axis=2)
    side_got = lon_halo(side_rims)
    inner = inner.at[:, :, 0].add(side_got[:, :, 0])
    inner = inner.at[:, :, -1].add(side_got[:, :, 3])
    middle = inner[:, 1:-1, :]
    north_rim = inner[:, -1, :]
    row_rims = jnp.stack([inner[:, 0, :], north_rim], axis=1)
    row_got = lat_halo(row_rims)
    middle = middle.at[:, 0, :].add(row_got[:, 0, :])
    middle = middle.at[:, -1, :].add(row_got[:, 3, :])
    is_top = top_flag()
    folded = jnp.where(is_top, signs[:, None] * north_rim[:, ::-1], 0.0)
    returned = mirror(folded)
    middle = middle.at[:, -1, :].add(jnp.where(is_top, returned, 0.0))
    return middle


def centred_x(field):
    return 0.5 * (field[1:-1, 2:] - field[1:-1, :-2])


def centred_y(field):
    return 0.5 * (field[2:, 1:-1] - field[:-2, 1:-1])


def stress_update(vel_pad, stress, strength, coef):
    east = vel_pad[0]
    north = vel_pad[1]
    dudx = centred_x(east)
    dudy = centred_y(east)
    dvdx = centred_x(north)
    dvdy = centred_y(north)
    diverge = dudx + dvdy
    tension = dudx - dvdy
    shearing = dudy + dvdx
    delta = jnp.sqrt(
        diverge * diverge + (tension * tension + shearing * shearing) / ellipse_sq + delta_floor
    )
    ratio = coef * strength / delta
    denom = 1.0 + coef
    first = (stress[0] + ratio * diverge - coef * strength) / denom
    second = (stress[1] + ratio * tension / ellipse_sq) / denom
    third = (stress[2] + ratio * shearing / ellipse_sq) / denom
    return jnp.stack([first, second, third], axis=0)


def velocity_update(stress_pad, velocity, wind, mass, land):
    first = stress_pad[0]
    second = stress_pad[1]
    third = stress_pad[2]
    force_x = 0.5 * centred_x(first + second) + centred_y(third)
    force_y = 0.5 * centred_y(first - second) + centred_x(third)
    scaled = land / (mass + time_step * drag_rate)
    east = scaled * (mass * velocity[0] + time_step * (force_x + wind[0]))
    north = scaled * (mass * velocity[1] + time_step * (force_y + wind[1]))
    return jnp.stack([east, north], axis=0)


def coefficient(start_index, step):
    return 0.2 + 0.8 * (start_index[0].astype(jnp.float32) + (step + 1)) / SUBTOTAL


def per_device(
    velocity, stress, wind, strength, mass, land_mask, region_mask, observed, start_index
):
    land = land_mask.astype(jnp.float32)
    region = region_mask.astype(jnp.float32)
    vel_signs = jnp.array([-1.0, -1.0], dtype=jnp.float32)
    stress_signs = jnp.array([1.0, 1.0, 1.0], dtype=jnp.float32)
    saved = []
    vel = velocity
    sts = stress
    for step in range(STEPS):
        coef = coefficient(start_index, step)
        vel_pad = extend(vel, vel_signs)
        new_sts = stress_update(vel_pad, sts, strength, coef)
        sts_pad = extend(new_sts, stress_signs)
        new_vel = velocity_update(sts_pad, vel, wind, mass, land)
        saved.append((vel, sts))
        vel = new_vel
        sts = new_sts
    vel_bar = region * (vel - observed)
    sts_bar = jnp.zeros_like(stress)
    wind_bar = jnp.zeros_like(wind)
    for step in reversed(range(STEPS)):
        coef = coefficient(start_index, step)
        old_vel, old_sts = saved[step]
        vel_pad = extend(old_vel, vel_signs)
        sts_pad = extend(stress_update(vel_pad, old_sts, strength, coef), stress_signs)

        def move_ice(stress_ext, speed, forcing):
            return velocity_update(stress_ext, speed, forcing, mass, land)

        def relax_stress(speed_ext, previous):
            return stress_update(speed_ext, previous, strength, coef)

        unused_vel, pull_velocity = jax.vjp(move_ice, sts_pad, old_vel, wind)
        stress_ext_bar, direct_bar, wind_part = pull_velocity(vel_bar)
        wind_bar = wind_bar + wind_part
        sts_bar = sts_bar + retract(stress_ext_bar, stress_signs)
        unused_sts, pull_stress = jax.vjp(relax_stress, vel_pad, old_sts)
        speed_ext_bar, sts_bar = pull_stress(sts_bar)
        vel_bar = direct_bar + retract(speed_ext_bar, vel_signs)
    total = lax.psum(jnp.sum(wind_bar * wind_bar), ("gx", "gy"))
    entries = 2 * wind_bar.shape[1] * wind_bar.shape[2] * lax.axis_size("gx") * lax.axis_size("gy")
    spread = jnp.sqrt(total / entries + norm_eps)
    state_adjoint = jnp.concatenate([vel_bar, sts_bar], axis=0)
    return (state_adjoint, wind_bar / spread)


def solution(mesh):
    return jax.shard_map(
        per_device,
        mesh=mesh,
        in_specs=(
            P(None, "gy", "gx"),
            P(None, "gy", "gx"),
            P(None, "gy", "gx"),
            P("gy", "gx"),
            P("gy", "gx"),
            P("gy", "gx"),
            P("gy", "gx"),
            P(None, "gy", "gx"),
            P(),
        ),
        out_specs=(P(None, "gy", "gx"), P(None, "gy", "gx")),
        check_vma=False,
    )
```

profile of v0, /device:TPU:0, one launch (start us, length us, event | category | flops | bytes accessed | tf_op | source)
XLA Modules:
  0.0 889.4 jit_solution(12096789865337416971)
XLA Ops:
  8.2 9.3 %all-gather = f32[2,1,1024]{2,1,0:T(1,128)S(1)} all-gather(f32[2,1,128]{2,1,0:T(1,128)S(1)} %get-tuple-element.1674), channel_id=2, replica_groups=mesh['gx'=8,'gy'=4] {'gx'}, dimensions={2}, use_global_device_ids=true | all-gather | bytes 9216 | tf_op jit(solution)/shard_map/all_gather | solution.py:41
  24.9 8.8 all-gather.1
  50.3 9.6 %all-gather.2 = f32[2,1,1024]{2,1,0:T(1,128)S(1)} all-gather(f32[2,1,128]{2,1,0:T(1,128)S(1)} %get-tuple-element.1672), channel_id=4, replica_groups=mesh['gx'=8,'gy'=4] {'gx'}, dimensions={2}, use_global_device_ids=true | all-gather | bytes 9216 | tf_op jit(solution)/shard_map/all_gather | solution.py:41
  75.7 8.8 all-gather.3
  153.9 9.4 %all-gather.6 = f32[2,1,1024]{2,1,0:T(1,128)S(1)} all-gather(f32[2,1,128]{2,1,0:T(1,128)S(1)} %get-tuple-element.1668), channel_id=8, replica_groups=mesh['gx'=8,'gy'=4] {'gx'}, dimensions={2}, use_global_device_ids=true | all-gather | bytes 9216 | tf_op jit(solution)/shard_map/all_gather | solution.py:41
  180.0 8.8 all-gather.7
  231.5 9.1 %all-gather.9 = f32[3,1,1024]{2,1,0:T(1,128)S(1)} all-gather(f32[3,1,128]{2,1,0:T(1,128)S(1)} %get-tuple-element.1593), channel_id=11, replica_groups=mesh['gx'=8,'gy'=4] {'gx'}, dimensions={2}, use_global_device_ids=true | all-gather | bytes 13824 | tf_op jit(solution)/shard_map/all_gather | solution.py:41
  258.4 9.2 %all-gather.10 = f32[2,1,1024]{2,1,0:T(1,128)S(1)} all-gather(f32[2,1,128]{2,1,0:T(1,128)S(1)} %get-tuple-element.1664), channel_id=12, replica_groups=mesh['gx'=8,'gy'=4] {'gx'}, dimensions={2}, use_global_device_ids=true | all-gather | bytes 9216 | tf_op jit(solution)/shard_map/all_gather | solution.py:41
  284.3 8.8 all-gather.11
  335.9 8.8 all-gather.13
  362.5 9.5 %all-gather.14 = f32[2,1,1024]{2,1,0:T(1,128)S(1)} all-gather(f32[2,1,128]{2,1,0:T(1,128)S(1)} %get-tuple-element.1660), channel_id=16, replica_groups=mesh['gx'=8,'gy'=4] {'gx'}, dimensions={2}, use_global_device_ids=true | all-gather | bytes 9216 | tf_op jit(solution)/shard_map/all_gather | solution.py:41
  388.7 8.8 all-gather.15
  446.3 9.1 %all_gather.121 = f32[2,1024]{1,0:T(2,128)S(1)} all-gather(f32[2,128]{1,0:T(2,128)S(1)} %multiply_select_fusion.7), channel_id=1, replica_groups=mesh['gx'=8,'gy'=4] {'gx'}, dimensions={1}, use_global_device_ids=true | all-gather | bytes 9216 | tf_op jit(solution)/shard_map/all_gather | solution.py:41
  470.3 9.8 %all_gather.122 = f32[3,1024]{1,0:T(4,128)S(1)} all-gather(f32[3,128]{1,0:T(4,128)S(1)} %broadcast_select_fusion.6), channel_id=1, replica_groups=mesh['gx'=8,'gy'=4] {'gx'}, dimensions={1}, use_global_device_ids=true | all-gather | bytes 13824 | tf_op jit(solution)/shard_map/all_gather | solution.py:41
  526.0 8.7 all_gather.124
  550.6 8.8 all_gather.125
  574.9 9.1 %all_gather.126 = f32[3,1024]{1,0:T(4,128)S(1)} all-gather(f32[3,128]{1,0:T(4,128)S(1)} %broadcast_select_fusion.4), channel_id=1, replica_groups=mesh['gx'=8,'gy'=4] {'gx'}, dimensions={1}, use_global_device_ids=true | all-gather | bytes 13824 | tf_op jit(solution)/shard_map/all_gather | solution.py:41
  638.4 8.8 all_gather.128
  690.4 8.8 all_gather.130
  724.6 8.6 all_gather.131
  787.3 8.8 all_gather.133
  796.9 40.4 %psum.7 = f32[]{:T(128)} all-reduce(f32[]{:T(128)} %get-tuple-element.1234), channel_id=1, replica_groups=mesh['gx'=8,'gy'=4] {'gx','gy'}, use_global_device_ids=true, to_apply=%region_1.2 | all-reduce | flops 1 | bytes 8 | tf_op jit(solution)/shard_map/psum | solution.py:165
  846.8 10.6 %all_gather.134 = f32[3,1024]{1,0:T(4,128)S(1)} all-gather(f32[3,128]{1,0:T(4,128)S(1)} %broadcast_select_fusion), channel_id=1, replica_groups=mesh['gx'=8,'gy'=4] {'gx'}, dimensions={1}, use_global_device_ids=true | all-gather | bytes 13824 | tf_op jit(solution)/shard_map/all_gather | solution.py:41
  873.9 8.8 all_gather.135
  (854 shorter events, 634.0 us)
Async XLA Ops:
  1.4 16.2 %collective-permute-start.1 = (f32[2,1,128]{2,0,1:T(2,128)S(1)}, f32[2,1,128]{2,0,1:T(2,128)S(1)}, u32[]{:S(2)}, u32[]{:S(2)}) collective-permute-start(f32[2,1,128]{2,0,1:T(2,128)S(1)} %bitcast.985), channel_id=1, source_target_pairs={{1,0},{2,1},{3,2},{5,4},{6,5},{7,6},{9,8},{10,9},{11,10},{13,12},{... | collective-permute-start | bytes 3080 | tf_op jit(solution)/shard_map/ppermute | solution.py:27
  2.6 15.0 %collective-permute-start = (f32[2,1,128]{2,1,0:T(1,128)S(1)}, f32[2,1,128]{2,1,0:T(1,128)S(1)}, u32[]{:S(2)}, u32[]{:S(2)}) collective-permute-start(f32[2,1,128]{2,1,0:T(1,128)S(1)} %get-tuple-element.1674), channel_id=1, source_target_pairs={{0,1},{1,2},{2,3},{4,5},{5,6},{6,7},{8,9},{9,10},{10,11},{12,13},{... | collective-permute-start | bytes 3080 | tf_op jit(solution)/shard_map/ppermute | solution.py:24
  420.7 10.8 %collective-permute-start.66 = (f32[3,1,128]{2,1,0:T(1,128)S(1)}, f32[3,1,128]{2,1,0:T(1,128)S(1)}, u32[]{:S(2)}, u32[]{:S(2)}) collective-permute-start(f32[3,1,128]{2,1,0:T(1,128)S(1)} %get-tuple-element.1558), channel_id=1, source_target_pairs={{0,1},{1,2},{2,3},{4,5},{5,6},{6,7},{8,9},{9,10},{10,11},{12,13},{... | collective-permute-start | bytes 4616 | tf_op jit(solution)/shard_map/ppermute | solution.py:24
  444.0 12.7 %collective-permute-start.70 = (f32[2,1,128]{2,1,0:T(1,128)S(1)}, f32[2,1,128]{2,1,0:T(1,128)S(1)}, u32[]{:S(2)}, u32[]{:S(2)}) collective-permute-start(f32[2,1,128]{2,1,0:T(1,128)S(1)} %get-tuple-element.1608), channel_id=1, source_target_pairs={{0,1},{1,2},{2,3},{4,5},{5,6},{6,7},{8,9},{9,10},{10,11},{12,13},{... | collective-permute-start | bytes 3080 | tf_op jit(solution)/shard_map/ppermute | solution.py:24
  468.2 13.1 %collective-permute-start.74 = (f32[3,1,128]{2,0,1:T(4,128)S(1)}, f32[3,1,128]{2,0,1:T(4,128)S(1)}, u32[]{:S(2)}, u32[]{:S(2)}) collective-permute-start(f32[3,1,128]{2,0,1:T(4,128)S(1)} %copy.1879), channel_id=1, source_target_pairs={{0,1},{1,2},{2,3},{4,5},{5,6},{6,7},{8,9},{9,10},{10,11},{12,13},{... | collective-permute-start | bytes 4616 | tf_op jit(solution)/shard_map/ppermute | solution.py:24
  502.5 11.5 %collective-permute-start.78 = (f32[2,1,128]{2,0,1:T(2,128)S(1)}, f32[2,1,128]{2,0,1:T(2,128)S(1)}, u32[]{:S(2)}, u32[]{:S(2)}) collective-permute-start(f32[2,1,128]{2,0,1:T(2,128)S(1)} %get-tuple-element.1639), channel_id=1, source_target_pairs={{0,1},{1,2},{2,3},{4,5},{5,6},{6,7},{8,9},{9,10},{10,11},{12,13},{... | collective-permute-start | bytes 3080 | tf_op jit(solution)/shard_map/ppermute | solution.py:24
  521.9 14.1 %collective-permute-start.82 = (f32[3,1,128]{2,0,1:T(4,128)S(1)}, f32[3,1,128]{2,0,1:T(4,128)S(1)}, u32[]{:S(2)}, u32[]{:S(2)}) collective-permute-start(f32[3,1,128]{2,0,1:T(4,128)S(1)} %copy.1878), channel_id=1, source_target_pairs={{0,1},{1,2},{2,3},{4,5},{5,6},{6,7},{8,9},{9,10},{10,11},{12,13},{... | collective-permute-start | bytes 4616 | tf_op jit(solution)/shard_map/ppermute | solution.py:24
  548.5 12.1 %collective-permute-start.86 = (f32[2,1,128]{2,1,0:T(1,128)S(1)}, f32[2,1,128]{2,1,0:T(1,128)S(1)}, u32[]{:S(2)}, u32[]{:S(2)}) collective-permute-start(f32[2,1,128]{2,1,0:T(1,128)S(1)} %get-tuple-element.1606), channel_id=1, source_target_pairs={{0,1},{1,2},{2,3},{4,5},{5,6},{6,7},{8,9},{9,10},{10,11},{12,13},{... | collective-permute-start | bytes 3080 | tf_op jit(solution)/shard_map/ppermute | solution.py:24
  572.3 13.1 %collective-permute-start.90 = (f32[3,1,128]{2,0,1:T(4,128)S(1)}, f32[3,1,128]{2,0,1:T(4,128)S(1)}, u32[]{:S(2)}, u32[]{:S(2)}) collective-permute-start(f32[3,1,128]{2,0,1:T(4,128)S(1)} %copy.1877), channel_id=1, source_target_pairs={{0,1},{1,2},{2,3},{4,5},{5,6},{6,7},{8,9},{9,10},{10,11},{12,13},{... | collective-permute-start | bytes 4616 | tf_op jit(solution)/shard_map/ppermute | solution.py:24
  606.3 11.5 %collective-permute-start.94 = (f32[2,1,128]{2,0,1:T(2,128)S(1)}, f32[2,1,128]{2,0,1:T(2,128)S(1)}, u32[]{:S(2)}, u32[]{:S(2)}) collective-permute-start(f32[2,1,128]{2,0,1:T(2,128)S(1)} %get-tuple-element.1636), channel_id=1, source_target_pairs={{0,1},{1,2},{2,3},{4,5},{5,6},{6,7},{8,9},{9,10},{10,11},{12,13},{... | collective-permute-start | bytes 3080 | tf_op jit(solution)/shard_map/ppermute | solution.py:24
  608.2 9.6 %collective-permute-start.95 = (f32[2,1,128]{2,0,1:T(2,128)S(1)}, f32[2,1,128]{2,0,1:T(2,128)S(1)}, u32[]{:S(2)}, u32[]{:S(2)}) collective-permute-start(f32[2,1,128]{2,0,1:T(2,128)S(1)} %get-tuple-element.1635), channel_id=1, source_target_pairs={{1,0},{2,1},{3,2},{5,4},{6,5},{7,6},{9,8},{10,9},{11,10},{13,12},{... | collective-permute-start | bytes 3080 | tf_op jit(solution)/shard_map/ppermute | solution.py:27
  633.0 14.2 %collective-permute-start.98 = (f32[3,1,128]{2,0,1:T(4,128)S(1)}, f32[3,1,128]{2,0,1:T(4,128)S(1)}, u32[]{:S(2)}, u32[]{:S(2)}) collective-permute-start(f32[3,1,128]{2,0,1:T(4,128)S(1)} %get-tuple-element.1517), channel_id=1, source_target_pairs={{0,1},{1,2},{2,3},{4,5},{5,6},{6,7},{8,9},{9,10},{10,11},{12,13},{... | collective-permute-start | bytes 4616 | tf_op jit(solution)/shard_map/ppermute | solution.py:24
  637.0 10.2 %collective-permute-start.99 = (f32[3,1,128]{2,0,1:T(4,128)S(1)}, f32[3,1,128]{2,0,1:T(4,128)S(1)}, u32[]{:S(2)}, u32[]{:S(2)}) collective-permute-start(f32[3,1,128]{2,0,1:T(4,128)S(1)} %get-tuple-element.1516), channel_id=1, source_target_pairs={{1,0},{2,1},{3,2},{5,4},{6,5},{7,6},{9,8},{10,9},{11,10},{13,12},{... | collective-permute-start | bytes 4616 | tf_op jit(solution)/shard_map/ppermute | solution.py:27
  663.9 14.3 %collective-permute-start.102 = (f32[2,1,128]{2,0,1:T(2,128)S(1)}, f32[2,1,128]{2,0,1:T(2,128)S(1)}, u32[]{:S(2)}, u32[]{:S(2)}) collective-permute-start(f32[2,1,128]{2,0,1:T(2,128)S(1)} %get-tuple-element.1633), channel_id=1, source_target_pairs={{0,1},{1,2},{2,3},{4,5},{5,6},{6,7},{8,9},{9,10},{10,11},{12,13},{... | collective-permute-start | bytes 3080 | tf_op jit(solution)/shard_map/ppermute | solution.py:24
  668.5 9.8 %collective-permute-start.103 = (f32[2,1,128]{2,0,1:T(2,128)S(1)}, f32[2,1,128]{2,0,1:T(2,128)S(1)}, u32[]{:S(2)}, u32[]{:S(2)}) collective-permute-start(f32[2,1,128]{2,0,1:T(2,128)S(1)} %get-tuple-element.1632), channel_id=1, source_target_pairs={{1,0},{2,1},{3,2},{5,4},{6,5},{7,6},{9,8},{10,9},{11,10},{13,12},{... | collective-permute-start | bytes 3080 | tf_op jit(solution)/shard_map/ppermute | solution.py:27
  685.9 14.6 %collective-permute-start.106 = (f32[3,1,128]{2,1,0:T(1,128)S(1)}, f32[3,1,128]{2,1,0:T(1,128)S(1)}, u32[]{:S(2)}, u32[]{:S(2)}) collective-permute-start(f32[3,1,128]{2,1,0:T(1,128)S(1)} %get-tuple-element.1547), channel_id=1, source_target_pairs={{0,1},{1,2},{2,3},{4,5},{5,6},{6,7},{8,9},{9,10},{10,11},{12,13},{... | collective-permute-start | bytes 4616 | tf_op jit(solution)/shard_map/ppermute | solution.py:24
  721.2 12.0 %collective-permute-start.110 = (f32[2,1,128]{2,0,1:T(2,128)S(1)}, f32[2,1,128]{2,0,1:T(2,128)S(1)}, u32[]{:S(2)}, u32[]{:S(2)}) collective-permute-start(f32[2,1,128]{2,0,1:T(2,128)S(1)} %get-tuple-element.1630), channel_id=1, source_target_pairs={{0,1},{1,2},{2,3},{4,5},{5,6},{6,7},{8,9},{9,10},{10,11},{12,13},{... | collective-permute-start | bytes 3080 | tf_op jit(solution)/shard_map/ppermute | solution.py:24
  723.2 10.1 %collective-permute-start.111 = (f32[2,1,128]{2,0,1:T(2,128)S(1)}, f32[2,1,128]{2,0,1:T(2,128)S(1)}, u32[]{:S(2)}, u32[]{:S(2)}) collective-permute-start(f32[2,1,128]{2,0,1:T(2,128)S(1)} %get-tuple-element.1629), channel_id=1, source_target_pairs={{1,0},{2,1},{3,2},{5,4},{6,5},{7,6},{9,8},{10,9},{11,10},{13,12},{... | collective-permute-start | bytes 3080 | tf_op jit(solution)/shard_map/ppermute | solution.py:27
  751.3 14.4 %collective-permute-start.114 = (f32[3,1,128]{2,0,1:T(4,128)S(1)}, f32[3,1,128]{2,0,1:T(4,128)S(1)}, u32[]{:S(2)}, u32[]{:S(2)}) collective-permute-start(f32[3,1,128]{2,0,1:T(4,128)S(1)} %get-tuple-element.1510), channel_id=1, source_target_pairs={{0,1},{1,2},{2,3},{4,5},{5,6},{6,7},{8,9},{9,10},{10,11},{12,13},{... | collective-permute-start | bytes 4616 | tf_op jit(solution)/shard_map/ppermute | solution.py:24
  755.9 9.9 %collective-permute-start.115 = (f32[3,1,128]{2,0,1:T(4,128)S(1)}, f32[3,1,128]{2,0,1:T(4,128)S(1)}, u32[]{:S(2)}, u32[]{:S(2)}) collective-permute-start(f32[3,1,128]{2,0,1:T(4,128)S(1)} %get-tuple-element.1509), channel_id=1, source_target_pairs={{1,0},{2,1},{3,2},{5,4},{6,5},{7,6},{9,8},{10,9},{11,10},{13,12},{... | collective-permute-start | bytes 4616 | tf_op jit(solution)/shard_map/ppermute | solution.py:27
  781.3 14.7 %collective-permute-start.118 = (f32[2,1,128]{2,0,1:T(2,128)S(1)}, f32[2,1,128]{2,0,1:T(2,128)S(1)}, u32[]{:S(2)}, u32[]{:S(2)}) collective-permute-start(f32[2,1,128]{2,0,1:T(2,128)S(1)} %get-tuple-element.1627), channel_id=1, source_target_pairs={{0,1},{1,2},{2,3},{4,5},{5,6},{6,7},{8,9},{9,10},{10,11},{12,13},{... | collective-permute-start | bytes 3080 | tf_op jit(solution)/shard_map/ppermute | solution.py:24
  785.9 10.2 %collective-permute-start.119 = (f32[2,1,128]{2,0,1:T(2,128)S(1)}, f32[2,1,128]{2,0,1:T(2,128)S(1)}, u32[]{:S(2)}, u32[]{:S(2)}) collective-permute-start(f32[2,1,128]{2,0,1:T(2,128)S(1)} %get-tuple-element.1626), channel_id=1, source_target_pairs={{1,0},{2,1},{3,2},{5,4},{6,5},{7,6},{9,8},{10,9},{11,10},{13,12},{... | collective-permute-start | bytes 3080 | tf_op jit(solution)/shard_map/ppermute | solution.py:27
  844.8 13.9 %collective-permute-start.122 = (f32[3,1,128]{2,1,0:T(1,128)S(1)}, f32[3,1,128]{2,1,0:T(1,128)S(1)}, u32[]{:S(2)}, u32[]{:S(2)}) collective-permute-start(f32[3,1,128]{2,1,0:T(1,128)S(1)} %get-tuple-element.1545), channel_id=1, source_target_pairs={{0,1},{1,2},{2,3},{4,5},{5,6},{6,7},{8,9},{9,10},{10,11},{12,13},{... | collective-permute-start | bytes 4616 | tf_op jit(solution)/shard_map/ppermute | solution.py:24
  871.2 12.8 %collective-permute-start.126 = (f32[2,1,128]{2,1,0:T(1,128)S(1)}, f32[2,1,128]{2,1,0:T(1,128)S(1)}, u32[]{:S(2)}, u32[]{:S(2)}) collective-permute-start(f32[2,1,128]{2,1,0:T(1,128)S(1)} %get-tuple-element.1604), channel_id=1, source_target_pairs={{0,1},{1,2},{2,3},{4,5},{5,6},{6,7},{8,9},{9,10},{10,11},{12,13},{... | collective-permute-start | bytes 3080 | tf_op jit(solution)/shard_map/ppermute | solution.py:24
  (113 other events, 604.8 us)
where the time goes:
time: 902 us; the launch traced here: 889 us
  blocking collectives  321 us (36%)
  waiting for transfers between devices  215 us (24%)
  starting transfers between devices  193 us (21%)
  local copies, waits for them, and re-layouts  113 us (13%)
  other arithmetic  41.3 us (5%)
    all_gather x32, blocking collectives, mirror(): whole = lax.all_gather(row, 'gx', axis=1, tiled=True)  280 us
    ppermute x64, waiting for transfers between devices, with_halo(): lax.ppermute(lax.slice_in_dim(block, block.shape[dim] - width, None, axis...  110 us
    ppermute x64, waiting for transfers between devices, with_halo(): lax.ppermute(lax.slice_in_dim(block, 0, width, axis=dim), axis, backward)  105 us
    ppermute x64, starting transfers between devices, with_halo(): lax.ppermute(lax.slice_in_dim(block, 0, width, axis=dim), axis, backward)  104 us
    ppermute x64, starting transfers between devices, with_halo(): lax.ppermute(lax.slice_in_dim(block, block.shape[dim] - width, None, axis...  88.2 us
    scatter-add x16, local copies, waits for them, and re-layouts, retract(): inner = inner.at[:, :, -1].add(side_got[:, :, 3])  57.9 us
    psum x1, blocking collectives, per_device(): total = lax.psum(jnp.sum(wind_bar * wind_bar), ('gx', 'gy'))  40.4 us
    concatenate x32, other arithmetic, with_halo(): block = jnp.concatenate([low, block, high], axis=dim)  23 us
  transfers between devices with their start and end apart: 128, of which 60 were waited for; matrix products, arithmetic and copies ran while one was open for 3% of the time, Pallas kernels for 0%

commit v1 on v0

v1 whole, which is shorter than its diff:
```python
import functools

import jax
import jax.numpy as jnp
from jax import lax
from jax.experimental import pallas as pl
from jax.experimental.pallas import tpu as pltpu
from jax.sharding import PartitionSpec as P

STEPS = 8
SUBTOTAL = 120
HALF = STEPS // 2
HALO = 4 * STEPS
COST_HALO = 2 * STEPS
PAD = 8
NORM_EPS = 1e-06
NF = 13
MESH = pl.DeviceIdType.MESH

U, V, G, M, T, WX, WY, STR, MASS, LAND, REGION, OBU, OBV = range(NF)
A, B8 = MASS, LAND
PH, QH, X1, X2, X3 = OBU, OBV, WX, WY, REGION
SW, SE, NW, NE = range(4)


def groups_of(chunks):
    per = 4
    body = list(range(per, chunks - per))
    mid = [body[i : i + per] for i in range(0, len(body), per)]
    return [list(range(per))] + mid + [list(range(chunks - per, chunks))]


def kernel(
    nx, ny, rows,
    start_ref, vel, sts, wind, strength, mass, land, region, obs,
    state_out, wind_out,
    F, IM, SB, RB, RC, SV, WB, CO, RED1, RED2,
    local_sem, send_sem, recv_sem, red_send, red_recv1, red_recv2,
):
    gx = lax.axis_index("gx")
    gy = lax.axis_index("gy")
    top = gy == ny - 1
    south_most = gy == 0
    lanes = F.shape[3]
    strip = HALO
    per = lanes // strip
    mid = PAD + HALO
    north = mid + rows
    east = lax.rem(gx + 1, nx)
    west = lax.rem(gx + nx - 1, nx)

    barrier = pltpu.get_barrier_semaphore()

    def greet(x, y):
        pl.semaphore_signal(barrier, inc=1, device_id={"gx": x, "gy": y}, device_id_type=MESH)

    for d in range(1, nx):
        greet(lax.rem(gx + d, nx), gy)
    for d in range(1, ny):
        greet(gx, lax.rem(gy + d, ny))

    @pl.when(gy < ny - 1)
    def _():
        greet(east, gy + 1)
        greet(west, gy + 1)

    @pl.when(gy > 0)
    def _():
        greet(east, gy - 1)
        greet(west, gy - 1)

    plan = [
        (vel, U, 2, HALO), (sts, G, 3, HALO), (wind, WX, 2, HALO), (strength, STR, 0, HALO),
        (mass, MASS, 0, HALO), (land, 0, -1, HALO), (region, 1, -1, COST_HALO),
        (obs, OBU, 2, COST_HALO),
    ]

    def src_rows(ref, count, first, n):
        return ref.at[:, pl.ds(first, n), :] if count > 0 else ref.at[pl.ds(first, n), :]

    def dst_rows(slot, count, first, n):
        if count > 0:
            return F.at[0, pl.ds(slot, count), pl.ds(first, n), :]
        if count == 0:
            return F.at[0, slot, pl.ds(first, n), :]
        return IM.at[slot, pl.ds(first, n), :]

    locals_ = []
    for i, (ref, slot, count, _) in enumerate(plan):
        copy = pltpu.make_async_copy(
            src_rows(ref, count, 0, rows), dst_rows(slot, count, mid, rows), local_sem.at[i]
        )
        copy.start()
        locals_.append(copy)

    start = start_ref[0].astype(jnp.float32)
    for k in range(STEPS):
        c = 0.2 + 0.8 * (jnp.full((8, lanes), start, jnp.float32) + (k + 1)) / SUBTOTAL
        inv = 1.0 / (1.0 + c)
        CO[k, 0] = inv
        CO[k, 1] = c * inv

    n_plan = len(plan)
    diag = jnp.where(top, 2, 4) - jnp.where(south_most, 2, 0)
    pl.semaphore_wait(barrier, nx - 1 + ny - 1 + diag)

    up_x = jnp.where(top, nx - 1 - gx, gx)
    up_y = jnp.where(top, gy, gy + 1)
    up_row = jnp.where(top, north, PAD)
    up_copies, down_copies = [], []
    for i, (ref, slot, count, width) in enumerate(plan):
        first = pl.multiple_of(up_row + (HALO - width), 8)
        up_copies.append(pltpu.make_async_remote_copy(
            src_ref=src_rows(ref, count, rows - width, width),
            dst_ref=dst_rows(slot, count, first, width),
            send_sem=send_sem.at[i],
            recv_sem=recv_sem.at[jnp.where(top, n_plan + i, i)],
            device_id={"gx": up_x, "gy": up_y}, device_id_type=MESH,
        ))
        down_copies.append(pltpu.make_async_remote_copy(
            src_ref=src_rows(ref, count, 0, width),
            dst_ref=dst_rows(slot, count, north, width),
            send_sem=send_sem.at[n_plan + i],
            recv_sem=recv_sem.at[n_plan + i],
            device_id={"gx": gx, "gy": jnp.maximum(gy - 1, 0)}, device_id_type=MESH,
        ))
    for copy in up_copies:
        copy.start()

    @pl.when(gy > 0)
    def _():
        for copy in down_copies:
            copy.start()

    for copy in locals_:
        copy.wait()

    lane = lax.broadcasted_iota(jnp.int32, (8, lanes), 1)
    part = lane // strip
    is_first = lane == 0
    is_last = lane == lanes - 1
    chunks = rows // 8
    groups = groups_of(chunks)

    def own(f, r):
        if f == LAND:
            return IM[0, pl.ds(r, 8), :].astype(jnp.float32)
        if f == REGION:
            return IM[1, pl.ds(r, 8), :].astype(jnp.float32)
        return F[0, f, pl.ds(r, 8), :]

    def spin(x, shift):
        shift = shift % lanes
        return pltpu.roll(x, shift, 1) if shift else x

    for f in range(NF):
        for g, members in enumerate(groups):
            block = [own(f, mid + 8 * c) for c in members]
            for side in range(2):
                out = None
                for q, x in enumerate(block):
                    y = spin(x, strip * (q + 1) if side == 0 else strip * q)
                    out = y if out is None else jnp.where(part == q, y, out)
                SB[side, f, pl.ds(8 * g, 8), :] = out

    n_groups = len(groups)
    base = 2 * n_plan
    tall = pl.ds(8 * (n_groups - 1), 8)
    short = pl.ds(0, 8)

    def remote(src, dst, s, r, x, y):
        return pltpu.make_async_remote_copy(
            src_ref=src, dst_ref=dst, send_sem=send_sem.at[s], recv_sem=recv_sem.at[r],
            device_id={"gx": x, "gy": y}, device_id_type=MESH,
        )

    side_e = remote(SB.at[0], RB.at[0], base, base, east, gy)
    side_w = remote(SB.at[1], RB.at[1], base + 1, base + 1, west, gy)
    up_ex = jnp.where(top, nx - 1 - east, east)
    up_wx = jnp.where(top, nx - 1 - west, west)
    ce = jnp.where(top, NW, SW)
    cw = jnp.where(top, NE, SE)
    corner_ue = remote(SB.at[0, :, tall, :], RC.at[ce], base + 2, base + 2 + ce, up_ex, up_y)
    corner_uw = remote(SB.at[1, :, tall, :], RC.at[cw], base + 3, base + 2 + cw, up_wx, up_y)
    self_e = pltpu.make_async_copy(SB.at[0, :, tall, :], RC.at[NW], recv_sem.at[base + 2 + NW])
    self_w = pltpu.make_async_copy(SB.at[1, :, tall, :], RC.at[NE], recv_sem.at[base + 2 + NE])
    down_y = jnp.maximum(gy - 1, 0)
    corner_de = remote(SB.at[0, :, short, :], RC.at[NW], base + 4, base + 2 + NW, east, down_y)
    corner_dw = remote(SB.at[1, :, short, :], RC.at[NE], base + 5, base + 2 + NE, west, down_y)
    to_self_e = jnp.logical_and(top, up_ex == gx)
    to_self_w = jnp.logical_and(top, up_wx == gx)

    def either(cond, yes, no):
        pl.when(cond)(yes)
        pl.when(jnp.logical_not(cond))(no)

    side_e.start()
    side_w.start()
    either(to_self_e, self_e.start, corner_ue.start)
    either(to_self_w, self_w.start, corner_uw.start)

    @pl.when(gy > 0)
    def _():
        corner_de.start()
        corner_dw.start()

    side_e.wait_recv()
    side_w.wait_recv()

    def arrived(dst, r):
        remote(dst, dst, 0, r, east, gy).wait_recv()

    @pl.when(gy > 0)
    def _():
        for i, (ref, slot, count, width) in enumerate(plan):
            arrived(dst_rows(slot, count, PAD + HALO - width, width), i)
        arrived(RC.at[SW], base + 2 + SW)
        arrived(RC.at[SE], base + 2 + SE)

    def north_rows(offset):
        for i, (ref, slot, count, width) in enumerate(plan):
            shift = HALO - width if offset else 0
            arrived(dst_rows(slot, count, north + shift, width), n_plan + i)

    either(top, lambda: north_rows(True), lambda: north_rows(False))

    def corner_wait(cond, copy, slot):
        either(cond, copy.wait, lambda: arrived(RC.at[slot], base + 2 + slot))

    corner_wait(to_self_e, self_e, NW)
    corner_wait(to_self_w, self_w, NE)

    for slot, f in ((0, LAND), (1, REGION)):
        for r in range(PAD, north + HALO, 8):
            F[0, f, pl.ds(r, 8), :] = IM[slot, pl.ds(r, 8), :].astype(jnp.float32)

    low = lane < lanes // 2

    def unpack(f, r, q, from_w, from_e):
        F[1, f, pl.ds(r, 8), :] = jnp.where(
            low, spin(from_e, -strip * q), spin(from_w, -strip * (q + 1))
        )

    for f in range(NF):
        for g, members in enumerate(groups):
            from_w = RB[0, f, pl.ds(8 * g, 8), :]
            from_e = RB[1, f, pl.ds(8 * g, 8), :]
            for q, c in enumerate(members):
                unpack(f, mid + 8 * c, q, from_w, from_e)
        for q in range(HALO // 8):
            unpack(f, PAD + 8 * q, q, RC[SW, f], RC[SE, f])
            unpack(f, north + 8 * q, q, RC[NW, f], RC[NE, f])

    @pl.when(south_most)
    def _():
        for col in range(2):
            for f in range(NF):
                for r in range(PAD, mid, 8):
                    F[col, f, pl.ds(r, 8), :] = jnp.zeros((8, lanes), jnp.float32)

    @pl.when(top)
    def _():
        flip_lane = lanes - 1 - lane
        flip_row = 7 - lax.broadcasted_iota(jnp.int32, (8, lanes), 0)

        def flip(x):
            x = jnp.take_along_axis(x, flip_lane, axis=1, mode="promise_in_bounds")
            return jnp.take_along_axis(x, flip_row, axis=0, mode="promise_in_bounds")

        n = HALO // 8
        for col in range(2):
            for f in range(NF):
                sign = -1.0 if f in (U, V, WX, WY, OBU, OBV) else 1.0
                block = [flip(F[col, f, pl.ds(north + 8 * q, 8), :]) for q in range(n)]
                for q in range(n):
                    F[col, f, pl.ds(north + 8 * (n - 1 - q), 8), :] = sign * block[q]

    def load(col, f, r):
        return F[col, f, pl.ds(r, 8), :]

    def save(col, f, r, value):
        F[col, f, pl.ds(r, 8), :] = value

    for r in range(PAD, north + HALO, 8):
        for col in range(2):
            m = load(col, MASS, r)
            scaled = load(col, LAND, r) / (m + 0.5)
            save(col, A, r, scaled * m)
            save(col, B8, r, 0.0625 * scaled)
            quarter = 0.25 * scaled
            save(col, WX, r, quarter * load(col, WX, r))
            save(col, WY, r, quarter * load(col, WY, r))
            save(col, U, r, 0.5 * load(col, U, r))
            save(col, V, r, 0.5 * load(col, V, r))
            s1 = load(col, G, r)
            s2 = load(col, M, r)
            save(col, G, r, 2.0 * (s1 + s2))
            save(col, M, r, 2.0 * (s1 - s2))
            save(col, T, r, 2.0 * load(col, T, r))

    def xdiff(f, r):
        c, e = load(0, f, r), load(1, f, r)
        lo_c = pltpu.roll(jnp.where(is_last, e, c), 1, 1)
        lo_e = pltpu.roll(jnp.where(is_last, c, e), 1, 1)
        hi_c = pltpu.roll(jnp.where(is_first, e, c), lanes - 1, 1)
        hi_e = pltpu.roll(jnp.where(is_first, c, e), lanes - 1, 1)
        return hi_c - lo_c, hi_e - lo_e

    def ydiff(f, r):
        return [load(col, f, r + 1) - load(col, f, r - 1) for col in range(2)]

    sv_lo = PAD + HALO - COST_HALO
    sv_hi = north + COST_HALO

    def forward(k, lo, hi):
        inv, kap = CO[k, 0], CO[k, 1]
        for r in range(lo, hi, 8):
            ux, vx, uy, vy = xdiff(U, r), xdiff(V, r), ydiff(U, r), ydiff(V, r)
            for col in range(2):
                d = ux[col] + vy[col]
                t = ux[col] - vy[col]
                s = uy[col] + vx[col]
                d2 = d + d
                i2 = lax.rsqrt(d2 * d2 + t * t + s * s + 0.16)
                a, b, e = d2 * i2, t * i2, s * i2
                q = kap * load(col, STR, r)
                am = a + a - 2.0
                save(col, G, r, inv * load(col, G, r) + q * (am + b))
                save(col, M, r, inv * load(col, M, r) + q * (am - b))
                save(col, T, r, inv * load(col, T, r) + q * e)
                if sv_lo <= r < sv_hi:
                    at = pl.ds(r - sv_lo, 8)
                    SV[k, col, 0, at, :] = a
                    SV[k, col, 1, at, :] = b
                    SV[k, col, 2, at, :] = e
                    SV[k, col, 3, at, :] = q * i2
        for r in range(lo, hi, 8):
            gxd, txd, td, md = xdiff(G, r), xdiff(T, r), ydiff(T, r), ydiff(M, r)
            for col in range(2):
                a, b = load(col, A, r), load(col, B8, r)
                save(col, U, r, a * load(col, U, r) + load(col, WX, r)
                     + b * (0.5 * gxd[col] + td[col]))
                save(col, V, r, a * load(col, V, r) + load(col, WY, r)
                     + b * (0.5 * md[col] + txd[col]))

    def run(first, count, step):
        def body(i, carry):
            step(first + i)
            return carry
        lax.fori_loop(0, count, body, 0)

    quarter_halo = HALO // 4
    run(0, HALF, lambda k: forward(k, PAD, north + HALO))
    run(HALF, HALF, lambda k: forward(k, PAD + quarter_halo, north + HALO - quarter_halo))

    for r in range(sv_lo, sv_hi, 8):
        for col in range(2):
            reg = load(col, REGION, r)
            b = load(col, B8, r)
            reg2 = reg + reg
            for f, o in ((U, OBU), (V, OBV)):
                x = load(col, f, r)
                bar = reg2 * (x + x - load(col, o, r))
                save(col, f, r, bar)
                save(col, o, r, b * bar)
            for f in (G, M, T):
                save(col, f, r, jnp.zeros((8, lanes), jnp.float32))
    for r in range(0, rows, 8):
        for f in range(2):
            WB[f, pl.ds(r, 8), :] = jnp.zeros((8, lanes), jnp.float32)

    def back_stress(k, lo, hi, count_wind, emit=False):
        inv = CO[k, 0]
        for r in range(lo, hi, 8):
            px, qx, py, qy = xdiff(PH, r), xdiff(QH, r), ydiff(PH, r), ydiff(QH, r)
            if count_wind and mid <= r < north:
                at = pl.ds(r - mid, 8)
                WB[0, at, :] = WB[0, at, :] + load(0, PH, r)
                WB[1, at, :] = WB[1, at, :] + load(0, QH, r)
            for col in range(2):
                at = pl.ds(r - sv_lo, 8)
                a, b, e, w = (SV[k, col, j, at, :] for j in range(4))
                t1 = load(col, G, r) - (px[col] + qy[col])
                t2 = load(col, M, r) - 0.5 * (px[col] - qy[col])
                t3 = load(col, T, r) - (py[col] + qx[col])
                kk = t1 * a + t2 * b + t3 * e
                z = t1 - kk * a
                z2 = z + z
                y2 = t2 - kk * b
                y3 = t3 - kk * e
                save(col, X1, r, w * (z2 + y2))
                save(col, X2, r, w * (z2 - y2))
                save(col, X3, r, w * y3)
                t1, t2, t3 = inv * t1, inv * t2, inv * t3
                if not emit:
                    save(col, G, r, t1)
                    save(col, M, r, t2)
                    save(col, T, r, t3)
                elif col == 0 and mid <= r < north:
                    at = pl.ds(r - mid, 8)
                    state_out[2, at, :] = t1
                    state_out[3, at, :] = t2 + t2
                    state_out[4, at, :] = t3 + t3

    def back_velocity(lo, hi, emit=False):
        for r in range(lo, hi, 8):
            x1, x3, y2, y3 = xdiff(X1, r), xdiff(X3, r), ydiff(X2, r), ydiff(X3, r)
            for col in range(2):
                if emit and col:
                    continue
                a = load(col, A, r)
                ub = a * load(col, U, r) - (x1[col] + y3[col])
                vb = a * load(col, V, r) - (y2[col] + x3[col])
                if emit:
                    at = pl.ds(r - mid, 8)
                    state_out[0, at, :] = 0.5 * ub
                    state_out[1, at, :] = 0.5 * vb
                else:
                    b = load(col, B8, r)
                    save(col, U, r, ub)
                    save(col, V, r, vb)
                    save(col, PH, r, b * ub)
                    save(col, QH, r, b * vb)

    def backward(k, lo, hi):
        back_stress(k, lo, hi, True)
        back_velocity(lo, hi)

    run(0, HALF, lambda i: backward(STEPS - 1 - i, sv_lo, sv_hi))
    near_lo, near_hi = mid - quarter_halo, north + quarter_halo
    run(0, HALF - 1, lambda i: backward(HALF - 1 - i, near_lo, near_hi))

    total = jnp.zeros((8, lanes), jnp.float32)
    for f, p in ((0, PH), (1, QH)):
        for r in range(0, rows, 8):
            at = pl.ds(r, 8)
            w = 4.0 * (WB[f, at, :] + load(0, p, mid + r))
            WB[f, at, :] = w
            total = total + w * w
    RED1[gx] = total
    row_sends = []
    for d in range(1, nx):
        row_sends.append(pltpu.make_async_remote_copy(
            src_ref=RED1.at[gx], dst_ref=RED1.at[gx], send_sem=red_send.at[d],
            recv_sem=red_recv1.at[d],
            device_id={"gx": lax.rem(gx + d, nx), "gy": gy}, device_id_type=MESH,
        ))
    for copy in row_sends:
        copy.start()

    back_stress(0, near_lo, near_hi, False, emit=True)

    def red_wait(ref, sem, d, n, here):
        slot = lax.rem(here + n - d, n)
        pltpu.make_async_remote_copy(
            src_ref=ref.at[slot], dst_ref=ref.at[slot], send_sem=red_send.at[d],
            recv_sem=sem.at[d], device_id={"gx": east, "gy": gy}, device_id_type=MESH,
        ).wait_recv()

    for d in range(1, nx):
        red_wait(RED1, red_recv1, d, nx, gx)
    total = RED1[0]
    for i in range(1, nx):
        total = total + RED1[i]
    RED2[gy] = total
    col_sends = []
    for d in range(1, ny):
        col_sends.append(pltpu.make_async_remote_copy(
            src_ref=RED2.at[gy], dst_ref=RED2.at[gy], send_sem=red_send.at[nx + d],
            recv_sem=red_recv2.at[d],
            device_id={"gx": gx, "gy": lax.rem(gy + d, ny)}, device_id_type=MESH,
        ))
    for copy in col_sends:
        copy.start()

    back_velocity(mid, north, emit=True)

    for d in range(1, ny):
        red_wait(RED2, red_recv2, d, ny, gy)
    total = RED2[0]
    for i in range(1, ny):
        total = total + RED2[i]
    entries = 2 * rows * lanes * nx * ny
    whole = jnp.sum(jnp.sum(total, axis=1, keepdims=True), axis=0, keepdims=True)
    spread = jnp.broadcast_to(whole, (8, lanes)) * (1.0 / entries) + NORM_EPS
    scale = 1.0 / jnp.sqrt(spread)
    for f in range(2):
        for r in range(0, rows, 8):
            at = pl.ds(r, 8)
            wind_out[f, at, :] = WB[f, at, :] * scale

    for copy in row_sends + col_sends + up_copies:
        copy.wait_send()
    side_e.wait_send()
    side_w.wait_send()
    pl.when(jnp.logical_not(to_self_e))(corner_ue.wait_send)
    pl.when(jnp.logical_not(to_self_w))(corner_uw.wait_send)

    @pl.when(gy > 0)
    def _():
        for copy in down_copies:
            copy.wait_send()
        corner_de.wait_send()
        corner_dw.wait_send()


def solution(mesh):
    nx, ny = mesh.shape["gx"], mesh.shape["gy"]

    def per_device(vel, sts, wind, strength, mass, land, region, obs, start):
        rows, lanes = strength.shape
        ext = rows + 2 * HALO + 2 * PAD
        n_groups = len(groups_of(rows // 8))
        f32 = jnp.float32
        hbm = pl.BlockSpec(memory_space=pl.ANY)
        vm = pl.BlockSpec(memory_space=pltpu.VMEM)
        return pl.pallas_call(
            functools.partial(kernel, nx, ny, rows),
            out_shape=(
                jax.ShapeDtypeStruct((5, rows, lanes), f32),
                jax.ShapeDtypeStruct((2, rows, lanes), f32),
            ),
            in_specs=[pl.BlockSpec(memory_space=pltpu.SMEM)] + [hbm] * 8,
            out_specs=(vm, vm),
            scratch_shapes=[
                pltpu.VMEM((2, NF, ext, lanes), f32),
                pltpu.VMEM((2, ext, lanes), jnp.int32),
                pltpu.VMEM((2, NF, 8 * n_groups, lanes), f32),
                pltpu.VMEM((2, NF, 8 * n_groups, lanes), f32),
                pltpu.VMEM((4, NF, 8, lanes), f32),
                pltpu.VMEM((STEPS, 2, 4, rows + 2 * COST_HALO, lanes), f32),
                pltpu.VMEM((2, rows, lanes), f32),
                pltpu.VMEM((STEPS, 2, 8, lanes), f32),
                pltpu.VMEM((nx, 8, lanes), f32),
                pltpu.VMEM((ny, 8, lanes), f32),
                pltpu.SemaphoreType.DMA((8,)),
                pltpu.SemaphoreType.DMA((22,)),
                pltpu.SemaphoreType.DMA((22,)),
                pltpu.SemaphoreType.DMA((nx + ny,)),
                pltpu.SemaphoreType.DMA((nx,)),
                pltpu.SemaphoreType.DMA((ny,)),
            ],
            compiler_params=pltpu.CompilerParams(
                collective_id=0, has_side_effects=True, vmem_limit_bytes=32 * 1024 * 1024
            ),
        )(start, vel, sts, wind, strength, mass, land, region, obs)

    block = P(None, "gy", "gx")
    flat = P("gy", "gx")
    return jax.shard_map(
        per_device,
        mesh=mesh,
        in_specs=(block, block, block, flat, flat, flat, flat, block, P()),
        out_specs=(block, block),
        check_vma=False,
    )
```

time: 902 us -> 41.1 us (0.05); the launches traced: 889 us -> 40.6 us
  blocking collectives: 321 us -> 0 us
  waiting for transfers between devices: 215 us -> 0 us
  starting transfers between devices: 193 us -> 0 us
  local copies, waits for them, and re-layouts: 113 us -> 7.98 us
  other arithmetic: 41.3 us -> 0 us
  Pallas kernels: 0 us -> 31.3 us
    all_gather x32 -> x0, blocking collectives: 280 us -> none  [mirror(): whole = lax.all_gather(row, 'gx', axis=1, tiled=True)]
    ppermute x128 -> x0, waiting for transfers between devices: 215 us -> none  [the longest x64 110 us: with_halo(): lax.ppermute(lax.slice_in_dim(block, block.shape[dim] - width, None, axis...]
    ppermute x128 -> x0, starting transfers between devices: 193 us -> none  [the longest x64 104 us: with_halo(): lax.ppermute(lax.slice_in_dim(block, 0, width, axis=dim), axis, backward)]
    scatter-add x67 -> x0, local copies, waits for them, and re-layouts: 73.6 us -> none  [the longest x16 57.9 us: retract(): inner = inner.at[:, :, -1].add(side_got[:, :, 3])]
    psum x1 -> x0, blocking collectives: 40.4 us -> none  [per_device(): total = lax.psum(jnp.sum(wind_bar * wind_bar), ('gx', 'gy'))]
    pallas_call x0 -> x1, Pallas kernels: none -> 31.3 us  [per_device(): pl.pallas_call(functools.partial(kernel, nx, ny, rows), out_shape=(jax.Sh...]
    concatenate x33 -> x0, other arithmetic: 23.7 us -> none  [the longest x32 23 us: with_halo(): block = jnp.concatenate([low, block, high], axis=dim)]
    scatter x16 -> x0, local copies, waits for them, and re-layouts: 15.9 us -> none  [extend(): rows = rows.at[:, -1, :].set(north)]
  transfers between devices with their start and end apart: 128 -> 0, of which waited for: 60 -> 0; matrix products, arithmetic and copies ran while one was open for 3% -> 0% of each run, Pallas kernels for 0% -> 0%
where the time goes in v1:
time: 41.1 us; the launch traced here: 40.6 us
  Pallas kernels  31.3 us (76%)
  local copies, waits for them, and re-layouts  7.98 us (19%)
  between operations  1.3 us (3%)
    pallas_call x1, Pallas kernels, per_device(): pl.pallas_call(functools.partial(kernel, nx, ny, rows), out_shape=(jax.Sh...  31.3 us
    unnamed x18, local copies, waits for them, and re-layouts  7.98 us

profile of v1, /device:TPU:0, one launch (start us, length us, event | category | flops | bytes accessed | tf_op | source)
XLA Modules:
  0.0 40.6 jit_solution(14832516112348142187)
XLA Ops:
  1.3 0.0 copy-start
  1.3 0.9 %copy-done = f32[3,80,128]{2,1,0:T(8,128)S(1)} copy-done((f32[3,80,128]{2,1,0:T(8,128)S(1)}, f32[3,80,128]{2,1,0:T(8,128)}, u32[]{:S(2)}) %copy-start) | copy-done | bytes 122904
  2.2 0.0 copy-start.1
  2.2 0.9 %copy-done.1 = f32[2,80,128]{2,1,0:T(8,128)S(1)} copy-done((f32[2,80,128]{2,1,0:T(8,128)S(1)}, f32[2,80,128]{2,1,0:T(8,128)}, u32[]{:S(2)}) %copy-start.1) | copy-done | bytes 81944
  3.1 0.0 copy-start.2
  3.1 0.9 %copy-done.2 = f32[2,80,128]{2,1,0:T(8,128)S(1)} copy-done((f32[2,80,128]{2,1,0:T(8,128)S(1)}, f32[2,80,128]{2,1,0:T(8,128)}, u32[]{:S(2)}) %copy-start.2) | copy-done | bytes 81944
  4.0 0.0 copy-start.3
  4.0 0.9 %copy-done.3 = f32[2,80,128]{2,1,0:T(8,128)S(1)} copy-done((f32[2,80,128]{2,1,0:T(8,128)S(1)}, f32[2,80,128]{2,1,0:T(8,128)}, u32[]{:S(2)}) %copy-start.3) | copy-done | bytes 81944
  4.8 0.0 copy-start.4
  4.8 0.8 %copy-done.4 = f32[80,128]{1,0:T(8,128)S(1)} copy-done((f32[80,128]{1,0:T(8,128)S(1)}, f32[80,128]{1,0:T(8,128)}, u32[]{:S(2)}) %copy-start.4) | copy-done | bytes 40984
  5.6 0.0 copy-start.5
  5.6 0.8 %copy-done.5 = f32[80,128]{1,0:T(8,128)S(1)} copy-done((f32[80,128]{1,0:T(8,128)S(1)}, f32[80,128]{1,0:T(8,128)}, u32[]{:S(2)}) %copy-start.5) | copy-done | bytes 40984
  6.4 0.0 copy-start.6
  6.4 0.8 %copy-done.6 = s32[80,128]{1,0:T(8,128)S(1)} copy-done((s32[80,128]{1,0:T(8,128)S(1)}, s32[80,128]{1,0:T(8,128)}, u32[]{:S(2)}) %copy-start.6) | copy-done | bytes 40984
  7.2 0.0 copy-start.7
  7.2 0.8 %copy-done.7 = s32[80,128]{1,0:T(8,128)S(1)} copy-done((s32[80,128]{1,0:T(8,128)S(1)}, s32[80,128]{1,0:T(8,128)}, u32[]{:S(2)}) %copy-start.7) | copy-done | bytes 40984
  8.0 31.3 %shard_map.104 = (f32[5,80,128]{2,1,0:T(8,128)S(1)}, f32[2,80,128]{2,1,0:T(8,128)S(1)}) custom-call(s32[1]{0:T(128)S(6)} %copy.13.start_ref, f32[2,80,128]{2,1,0:T(8,128)S(1)} %copy-done.1, f32[3,80,128]{2,1,0:T(8,128)S(1)} %copy-done, f32[2,80,128]{2,1,0:T(8,128)S(1)} %copy-done.2, f32[80,128]{1,0:T(8,128)S(1)} %copy-done.4, f32[80,128]{1,0:T(8,128)S(1)} %copy-done.5, ...), custom_call_target="tpu_custom_call" | custom-call | tf_op jit(solution)/shard_map/pallas_call | solution.py:517
  39.3 0.7 %copy.14 = f32[5,80,128]{2,1,0:T(8,128)} copy(f32[5,80,128]{2,1,0:T(8,128)S(1)} %get-tuple-element.4) | data formatting | bytes 409600
  40.0 0.6 %copy.15 = f32[2,80,128]{2,1,0:T(8,128)} copy(f32[2,80,128]{2,1,0:T(8,128)S(1)} %get-tuple-element.5) | data formatting | bytes 163840
Async XLA Ops:
  1.3 0.9 %copy-start = (f32[3,80,128]{2,1,0:T(8,128)S(1)}, f32[3,80,128]{2,1,0:T(8,128)}, u32[]{:S(2)}) copy-start(f32[3,80,128]{2,1,0:T(8,128)} %sts.1) | copy-start | bytes 368644
  2.2 0.9 %copy-start.1 = (f32[2,80,128]{2,1,0:T(8,128)S(1)}, f32[2,80,128]{2,1,0:T(8,128)}, u32[]{:S(2)}) copy-start(f32[2,80,128]{2,1,0:T(8,128)} %vel.1) | copy-start | bytes 245764
  3.1 0.9 %copy-start.2 = (f32[2,80,128]{2,1,0:T(8,128)S(1)}, f32[2,80,128]{2,1,0:T(8,128)}, u32[]{:S(2)}) copy-start(f32[2,80,128]{2,1,0:T(8,128)} %wind.1) | copy-start | bytes 245764
  4.0 0.9 %copy-start.3 = (f32[2,80,128]{2,1,0:T(8,128)S(1)}, f32[2,80,128]{2,1,0:T(8,128)}, u32[]{:S(2)}) copy-start(f32[2,80,128]{2,1,0:T(8,128)} %obs.1) | copy-start | bytes 245764
  4.8 0.8 %copy-start.4 = (f32[80,128]{1,0:T(8,128)S(1)}, f32[80,128]{1,0:T(8,128)}, u32[]{:S(2)}) copy-start(f32[80,128]{1,0:T(8,128)} %strength.1) | copy-start | bytes 122884
  5.6 0.8 %copy-start.5 = (f32[80,128]{1,0:T(8,128)S(1)}, f32[80,128]{1,0:T(8,128)}, u32[]{:S(2)}) copy-start(f32[80,128]{1,0:T(8,128)} %mass.1) | copy-start | bytes 122884
  6.4 0.8 %copy-start.6 = (s32[80,128]{1,0:T(8,128)S(1)}, s32[80,128]{1,0:T(8,128)}, u32[]{:S(2)}) copy-start(s32[80,128]{1,0:T(8,128)} %land.1) | copy-start | bytes 122884
  7.2 0.8 %copy-start.7 = (s32[80,128]{1,0:T(8,128)S(1)}, s32[80,128]{1,0:T(8,128)}, u32[]{:S(2)}) copy-start(s32[80,128]{1,0:T(8,128)} %region.1) | copy-start | bytes 122884

commit v2 on v1

--- a/solution.py
+++ b/solution.py
@@ -15,6 +15,7 @@
 PAD = 8
 NORM_EPS = 1e-06
 NF = 13
+NCRIT = 10
 MESH = pl.DeviceIdType.MESH
 
 U, V, G, M, T, WX, WY, STR, MASS, LAND, REGION, OBU, OBV = range(NF)
@@ -33,7 +34,7 @@
 def kernel(
     nx, ny, rows,
     start_ref, vel, sts, wind, strength, mass, land, region, obs,
-    state_out, wind_out,
+    out,
     F, IM, SB, RB, RC, SV, WB, CO, RED1, RED2,
     local_sem, send_sem, recv_sem, red_send, red_recv1, red_recv2,
 ):
@@ -124,13 +125,18 @@
             recv_sem=recv_sem.at[n_plan + i],
             device_id={"gx": gx, "gy": jnp.maximum(gy - 1, 0)}, device_id_type=MESH,
         ))
-    for copy in up_copies:
-        copy.start()
-
-    @pl.when(gy > 0)
-    def _():
-        for copy in down_copies:
+    late = 6
+
+    def start_rows(lo, hi):
+        for copy in up_copies[lo:hi]:
             copy.start()
+
+        @pl.when(gy > 0)
+        def _():
+            for copy in down_copies[lo:hi]:
+                copy.start()
+
+    start_rows(0, late)
 
     for copy in locals_:
         copy.wait()
@@ -157,11 +163,11 @@
         for g, members in enumerate(groups):
             block = [own(f, mid + 8 * c) for c in members]
             for side in range(2):
-                out = None
+                packed = None
                 for q, x in enumerate(block):
                     y = spin(x, strip * (q + 1) if side == 0 else strip * q)
-                    out = y if out is None else jnp.where(part == q, y, out)
-                SB[side, f, pl.ds(8 * g, 8), :] = out
+                    packed = y if packed is None else jnp.where(part == q, y, packed)
+                SB[side, f, pl.ds(8 * g, 8), :] = packed
 
     n_groups = len(groups)
     base = 2 * n_plan
@@ -174,19 +180,11 @@
             device_id={"gx": x, "gy": y}, device_id_type=MESH,
         )
 
-    side_e = remote(SB.at[0], RB.at[0], base, base, east, gy)
-    side_w = remote(SB.at[1], RB.at[1], base + 1, base + 1, west, gy)
+    down_y = jnp.maximum(gy - 1, 0)
     up_ex = jnp.where(top, nx - 1 - east, east)
     up_wx = jnp.where(top, nx - 1 - west, west)
     ce = jnp.where(top, NW, SW)
     cw = jnp.where(top, NE, SE)
-    corner_ue = remote(SB.at[0, :, tall, :], RC.at[ce], base + 2, base + 2 + ce, up_ex, up_y)
-    corner_uw = remote(SB.at[1, :, tall, :], RC.at[cw], base + 3, base + 2 + cw, up_wx, up_y)
-    self_e = pltpu.make_async_copy(SB.at[0, :, tall, :], RC.at[NW], recv_sem.at[base + 2 + NW])
-    self_w = pltpu.make_async_copy(SB.at[1, :, tall, :], RC.at[NE], recv_sem.at[base + 2 + NE])
-    down_y = jnp.maximum(gy - 1, 0)
-    corner_de = remote(SB.at[0, :, short, :], RC.at[NW], base + 4, base + 2 + NW, east, down_y)
-    corner_dw = remote(SB.at[1, :, short, :], RC.at[NE], base + 5, base + 2 + NE, west, down_y)
     to_self_e = jnp.logical_and(top, up_ex == gx)
     to_self_w = jnp.logical_and(top, up_wx == gx)
 
@@ -194,45 +192,81 @@
         pl.when(cond)(yes)
         pl.when(jnp.logical_not(cond))(no)
 
-    side_e.start()
-    side_w.start()
-    either(to_self_e, self_e.start, corner_ue.start)
-    either(to_self_w, self_w.start, corner_uw.start)
-
-    @pl.when(gy > 0)
-    def _():
-        corner_de.start()
-        corner_dw.start()
-
-    side_e.wait_recv()
-    side_w.wait_recv()
-
     def arrived(dst, r):
         remote(dst, dst, 0, r, east, gy).wait_recv()
 
-    @pl.when(gy > 0)
-    def _():
-        for i, (ref, slot, count, width) in enumerate(plan):
-            arrived(dst_rows(slot, count, PAD + HALO - width, width), i)
-        arrived(RC.at[SW], base + 2 + SW)
-        arrived(RC.at[SE], base + 2 + SE)
-
-    def north_rows(offset):
-        for i, (ref, slot, count, width) in enumerate(plan):
-            shift = HALO - width if offset else 0
-            arrived(dst_rows(slot, count, north + shift, width), n_plan + i)
-
-    either(top, lambda: north_rows(True), lambda: north_rows(False))
-
-    def corner_wait(cond, copy, slot):
-        either(cond, copy.wait, lambda: arrived(RC.at[slot], base + 2 + slot))
-
-    corner_wait(to_self_e, self_e, NW)
-    corner_wait(to_self_w, self_w, NE)
-
-    for slot, f in ((0, LAND), (1, REGION)):
-        for r in range(PAD, north + HALO, 8):
-            F[0, f, pl.ds(r, 8), :] = IM[slot, pl.ds(r, 8), :].astype(jnp.float32)
+    class Edges:
+        def __init__(self, f0, n, at):
+            fs = pl.ds(f0, n)
+            self.fs, self.at = fs, at
+            self.side_e = remote(SB.at[0, fs], RB.at[0, fs], at, at, east, gy)
+            self.side_w = remote(SB.at[1, fs], RB.at[1, fs], at + 1, at + 1, west, gy)
+            hi_e, hi_w = SB.at[0, fs, tall, :], SB.at[1, fs, tall, :]
+            lo_e, lo_w = SB.at[0, fs, short, :], SB.at[1, fs, short, :]
+            c = at + 2
+            self.up_e = remote(hi_e, RC.at[ce, fs], at + 2, c + ce, up_ex, up_y)
+            self.up_w = remote(hi_w, RC.at[cw, fs], at + 3, c + cw, up_wx, up_y)
+            self.self_e = pltpu.make_async_copy(hi_e, RC.at[NW, fs], recv_sem.at[c + NW])
+            self.self_w = pltpu.make_async_copy(hi_w, RC.at[NE, fs], recv_sem.at[c + NE])
+            self.down_e = remote(lo_e, RC.at[NW, fs], at + 4, c + NW, east, down_y)
+            self.down_w = remote(lo_w, RC.at[NE, fs], at + 5, c + NE, west, down_y)
+
+        def start(self):
+            either(to_self_e, self.self_e.start, self.up_e.start)
+            either(to_self_w, self.self_w.start, self.up_w.start)
+
+            @pl.when(gy > 0)
+            def _():
+                self.down_e.start()
+                self.down_w.start()
+
+            self.side_e.start()
+            self.side_w.start()
+
+        def wait_recv(self):
+            c = self.at + 2
+            self.side_e.wait_recv()
+            self.side_w.wait_recv()
+
+            @pl.when(gy > 0)
+            def _():
+                arrived(RC.at[SW, self.fs], c + SW)
+                arrived(RC.at[SE, self.fs], c + SE)
+
+            either(to_self_e, self.self_e.wait, lambda: arrived(RC.at[NW, self.fs], c + NW))
+            either(to_self_w, self.self_w.wait, lambda: arrived(RC.at[NE, self.fs], c + NE))
+
+        def wait_send(self):
+            self.side_e.wait_send()
+            self.side_w.wait_send()
+            pl.when(jnp.logical_not(to_self_e))(self.up_e.wait_send)
+            pl.when(jnp.logical_not(to_self_w))(self.up_w.wait_send)
+
+            @pl.when(gy > 0)
+            def _():
+                self.down_e.wait_send()
+                self.down_w.wait_send()
+
+    early_edges = Edges(0, NCRIT, base)
+    late_edges = Edges(NCRIT, NF - NCRIT, base + 6)
+    early_edges.start()
+    start_rows(late, n_plan)
+    late_edges.start()
+
+    def wait_rows(lo, hi):
+        @pl.when(gy > 0)
+        def _():
+            for i in range(lo, hi):
+                _, slot, count, width = plan[i]
+                arrived(dst_rows(slot, count, PAD + HALO - width, width), i)
+
+        def north_rows(folded):
+            for i in range(lo, hi):
+                _, slot, count, width = plan[i]
+                shift = HALO - width if folded else 0
+                arrived(dst_rows(slot, count, north + shift, width), n_plan + i)
+
+        either(top, lambda: north_rows(True), lambda: north_rows(False))
 
     low = lane < lanes // 2
 
@@ -241,39 +275,47 @@
             low, spin(from_e, -strip * q), spin(from_w, -strip * (q + 1))
         )
 
-    for f in range(NF):
-        for g, members in enumerate(groups):
-            from_w = RB[0, f, pl.ds(8 * g, 8), :]
-            from_e = RB[1, f, pl.ds(8 * g, 8), :]
-            for q, c in enumerate(members):
-                unpack(f, mid + 8 * c, q, from_w, from_e)
-        for q in range(HALO // 8):
-            unpack(f, PAD + 8 * q, q, RC[SW, f], RC[SE, f])
-            unpack(f, north + 8 * q, q, RC[NW, f], RC[NE, f])
-
-    @pl.when(south_most)
-    def _():
-        for col in range(2):
-            for f in range(NF):
-                for r in range(PAD, mid, 8):
-                    F[col, f, pl.ds(r, 8), :] = jnp.zeros((8, lanes), jnp.float32)
-
-    @pl.when(top)
-    def _():
-        flip_lane = lanes - 1 - lane
-        flip_row = 7 - lax.broadcasted_iota(jnp.int32, (8, lanes), 0)
-
-        def flip(x):
-            x = jnp.take_along_axis(x, flip_lane, axis=1, mode="promise_in_bounds")
-            return jnp.take_along_axis(x, flip_row, axis=0, mode="promise_in_bounds")
-
-        n = HALO // 8
-        for col in range(2):
-            for f in range(NF):
-                sign = -1.0 if f in (U, V, WX, WY, OBU, OBV) else 1.0
-                block = [flip(F[col, f, pl.ds(north + 8 * q, 8), :]) for q in range(n)]
-                for q in range(n):
-                    F[col, f, pl.ds(north + 8 * (n - 1 - q), 8), :] = sign * block[q]
+    def settle(fields, slot, mask):
+        for r in range(PAD, north + HALO, 8):
+            F[0, mask, pl.ds(r, 8), :] = IM[slot, pl.ds(r, 8), :].astype(jnp.float32)
+
+        for f in fields:
+            for g, members in enumerate(groups):
+                from_w = RB[0, f, pl.ds(8 * g, 8), :]
+                from_e = RB[1, f, pl.ds(8 * g, 8), :]
+                for q, c in enumerate(members):
+                    unpack(f, mid + 8 * c, q, from_w, from_e)
+            for q in range(HALO // 8):
+                unpack(f, PAD + 8 * q, q, RC[SW, f], RC[SE, f])
+                unpack(f, north + 8 * q, q, RC[NW, f], RC[NE, f])
+
+        @pl.when(south_most)
+        def _():
+            for col in range(2):
+                for f in fields:
+                    for r in range(PAD, mid, 8):
+                        F[col, f, pl.ds(r, 8), :] = jnp.zeros((8, lanes), jnp.float32)
+
+        @pl.when(top)
+        def _():
+            flip_lane = lanes - 1 - lane
+            flip_row = 7 - lax.broadcasted_iota(jnp.int32, (8, lanes), 0)
+
+            def flip(x):
+                x = jnp.take_along_axis(x, flip_lane, axis=1, mode="promise_in_bounds")
+                return jnp.take_along_axis(x, flip_row, axis=0, mode="promise_in_bounds")
+
+            n = HALO // 8
+            for col in range(2):
+                for f in fields:
+                    sign = -1.0 if f in (U, V, WX, WY, OBU, OBV) else 1.0
+                    block = [flip(F[col, f, pl.ds(north + 8 * q, 8), :]) for q in range(n)]
+                    for q in range(n):
+                        F[col, f, pl.ds(north + 8 * (n - 1 - q), 8), :] = sign * block[q]
+
+    early_edges.wait_recv()
+    wait_rows(0, late)
+    settle(range(NCRIT), 0, LAND)
 
     def load(col, f, r):
         return F[col, f, pl.ds(r, 8), :]
@@ -353,6 +395,10 @@
     run(0, HALF, lambda k: forward(k, PAD, north + HALO))
     run(HALF, HALF, lambda k: forward(k, PAD + quarter_halo, north + HALO - quarter_halo))
 
+    late_edges.wait_recv()
+    wait_rows(late, n_plan)
+    settle(range(NCRIT, NF), 1, REGION)
+
     for r in range(sv_lo, sv_hi, 8):
         for col in range(2):
             reg = load(col, REGION, r)
@@ -398,9 +444,9 @@
                     save(col, T, r, t3)
                 elif col == 0 and mid <= r < north:
                     at = pl.ds(r - mid, 8)
-                    state_out[2, at, :] = t1
-                    state_out[3, at, :] = t2 + t2
-                    state_out[4, at, :] = t3 + t3
+                    out[2, at, :] = t1
+                    out[3, at, :] = t2 + t2
+                    out[4, at, :] = t3 + t3
 
     def back_velocity(lo, hi, emit=False):
         for r in range(lo, hi, 8):
@@ -413,8 +459,8 @@
                 vb = a * load(col, V, r) - (y2[col] + x3[col])
                 if emit:
                     at = pl.ds(r - mid, 8)
-                    state_out[0, at, :] = 0.5 * ub
-                    state_out[1, at, :] = 0.5 * vb
+                    out[0, at, :] = 0.5 * ub
+                    out[1, at, :] = 0.5 * vb
                 else:
                     b = load(col, B8, r)
                     save(col, U, r, ub)
@@ -437,6 +483,7 @@
             w = 4.0 * (WB[f, at, :] + load(0, p, mid + r))
             WB[f, at, :] = w
             total = total + w * w
+    total = jnp.sum(total, axis=0, keepdims=True)
     RED1[gx] = total
     row_sends = []
     for d in range(1, nx):
@@ -481,27 +528,32 @@
     for i in range(1, ny):
         total = total + RED2[i]
     entries = 2 * rows * lanes * nx * ny
-    whole = jnp.sum(jnp.sum(total, axis=1, keepdims=True), axis=0, keepdims=True)
+    whole = jnp.sum(total, axis=1, keepdims=True)
     spread = jnp.broadcast_to(whole, (8, lanes)) * (1.0 / entries) + NORM_EPS
     scale = 1.0 / jnp.sqrt(spread)
     for f in range(2):
         for r in range(0, rows, 8):
             at = pl.ds(r, 8)
-            wind_out[f, at, :] = WB[f, at, :] * scale
+            out[5 + f, at, :] = WB[f, at, :] * scale
 
     for copy in row_sends + col_sends + up_copies:
         copy.wait_send()
-    side_e.wait_send()
-    side_w.wait_send()
-    pl.when(jnp.logical_not(to_self_e))(corner_ue.wait_send)
-    pl.when(jnp.logical_not(to_self_w))(corner_uw.wait_send)
+    early_edges.wait_send()
+    late_edges.wait_send()
 
     @pl.when(gy > 0)
     def _():
         for copy in down_copies:
             copy.wait_send()
-        corner_de.wait_send()
-        corner_dw.wait_send()
+
+
+def split_kernel(both, state_out, wind_out, sem):
+    one = pltpu.make_async_copy(both.at[pl.ds(0, 5)], state_out, sem.at[0])
+    two = pltpu.make_async_copy(both.at[pl.ds(5, 2)], wind_out, sem.at[1])
+    one.start()
+    two.start()
+    one.wait()
+    two.wait()
 
 
 def solution(mesh):
@@ -514,14 +566,15 @@
         f32 = jnp.float32
         hbm = pl.BlockSpec(memory_space=pl.ANY)
         vm = pl.BlockSpec(memory_space=pltpu.VMEM)
-        return pl.pallas_call(
+        vel, sts, wind, strength, mass, land, region, obs = (
+            pltpu.with_memory_space_constraint(x, pltpu.HBM)
+            for x in (vel, sts, wind, strength, mass, land, region, obs)
+        )
+        both = pl.pallas_call(
             functools.partial(kernel, nx, ny, rows),
-            out_shape=(
-                jax.ShapeDtypeStruct((5, rows, lanes), f32),
-                jax.ShapeDtypeStruct((2, rows, lanes), f32),
-            ),
+            out_shape=jax.ShapeDtypeStruct((7, rows, lanes), f32),
             in_specs=[pl.BlockSpec(memory_space=pltpu.SMEM)] + [hbm] * 8,
-            out_specs=(vm, vm),
+            out_specs=vm,
             scratch_shapes=[
                 pltpu.VMEM((2, NF, ext, lanes), f32),
                 pltpu.VMEM((2, ext, lanes), jnp.int32),
@@ -531,11 +584,11 @@
                 pltpu.VMEM((STEPS, 2, 4, rows + 2 * COST_HALO, lanes), f32),
                 pltpu.VMEM((2, rows, lanes), f32),
                 pltpu.VMEM((STEPS, 2, 8, lanes), f32),
-                pltpu.VMEM((nx, 8, lanes), f32),
-                pltpu.VMEM((ny, 8, lanes), f32),
+                pltpu.VMEM((nx, 1, lanes), f32),
+                pltpu.VMEM((ny, 1, lanes), f32),
                 pltpu.SemaphoreType.DMA((8,)),
-                pltpu.SemaphoreType.DMA((22,)),
-                pltpu.SemaphoreType.DMA((22,)),
+                pltpu.SemaphoreType.DMA((28,)),
+                pltpu.SemaphoreType.DMA((28,)),
                 pltpu.SemaphoreType.DMA((nx + ny,)),
                 pltpu.SemaphoreType.DMA((nx,)),
                 pltpu.SemaphoreType.DMA((ny,)),
@@ -544,6 +597,16 @@
                 collective_id=0, has_side_effects=True, vmem_limit_bytes=32 * 1024 * 1024
             ),
         )(start, vel, sts, wind, strength, mass, land, region, obs)
+        return pl.pallas_call(
+            split_kernel,
+            out_shape=(
+                jax.ShapeDtypeStruct((5, rows, lanes), f32),
+                jax.ShapeDtypeStruct((2, rows, lanes), f32),
+            ),
+            in_specs=[vm],
+            out_specs=(hbm, hbm),
+            scratch_shapes=[pltpu.SemaphoreType.DMA((2,))],
+        )(both)
 
     block = P(None, "gy", "gx")
     flat = P("gy", "gx")

time: 41.1 us -> 33.8 us (0.82)
  local copies, waits for them, and re-layouts: 7.98 us -> 0.7 us
    unnamed x18 -> x2, local copies, waits for them, and re-layouts: 7.98 us -> 0.7 us
    pallas_call x1 -> x2, Pallas kernels: 31.3 us -> 31.6 us  [the longest x1 29.9 us: per_device(): pl.pallas_call(functools.partial(kernel, nx, ny, rows), out_shape=jax.Sha...]
where the time goes in v2:
time: 33.8 us; the launch traced here: 33.6 us
  Pallas kernels  31.6 us (93%)
  between operations  1.3 us (4%)
  local copies, waits for them, and re-layouts  0.7 us (2%)
    pallas_call x1, Pallas kernels, per_device(): pl.pallas_call(functools.partial(kernel, nx, ny, rows), out_shape=jax.Sha...  29.9 us
    pallas_call x1, Pallas kernels, per_device(): pl.pallas_call(split_kernel, out_shape=(jax.ShapeDtypeStruct((5, rows, la...  1.68 us
    unnamed x2, local copies, waits for them, and re-layouts  0.7 us

profile of v2, /device:TPU:0, one launch (start us, length us, event | category | flops | bytes accessed | tf_op | source)
XLA Modules:
  0.0 33.6 jit_solution(14091079596775577456)
XLA Ops:
  1.3 29.9 %shard_map.104.both = f32[7,80,128]{2,1,0:T(8,128)S(1)} custom-call(s32[1]{0:T(128)S(6)} %copy.11.start_ref, f32[2,80,128]{2,1,0:T(8,128)} %vel.1, f32[3,80,128]{2,1,0:T(8,128)} %sts.1, f32[2,80,128]{2,1,0:T(8,128)} %wind.1, f32[80,128]{1,0:T(8,128)} %strength.1, f32[80,128]{1,0:T(8,128)} %mass.1, s32[80,128]{1,0:T(8,128)} %land.1, s32[80,128]{1,0:T(8,128)} %region.1, ...), custom_call_target="tpu_custom_call" | custom-call | tf_op jit(solution)/shard_map/pallas_call | solution.py:573
  31.2 0.0 copy-start
  31.2 0.7 %copy-done = f32[7,80,128]{2,1,0:T(8,128)} copy-done((f32[7,80,128]{2,1,0:T(8,128)}, f32[7,80,128]{2,1,0:T(8,128)S(1)}, u32[]{:S(2)}) %copy-start) | copy-done | bytes 286744
  31.9 1.7 %shard_map.105 = (f32[5,80,128]{2,1,0:T(8,128)}, f32[2,80,128]{2,1,0:T(8,128)}) custom-call(f32[7,80,128]{2,1,0:T(8,128)} %copy-done), custom_call_target="tpu_custom_call" | custom-call | tf_op jit(solution)/shard_map/pallas_call | solution.py:600
Async XLA Ops:
  31.2 0.7 %copy-start = (f32[7,80,128]{2,1,0:T(8,128)}, f32[7,80,128]{2,1,0:T(8,128)S(1)}, u32[]{:S(2)}) copy-start(f32[7,80,128]{2,1,0:T(8,128)S(1)} %shard_map.104.both) | copy-start | bytes 860164

commit v3 on v2

--- a/solution.py
+++ b/solution.py
@@ -223,10 +223,12 @@
             self.side_e.start()
             self.side_w.start()
 
-        def wait_recv(self):
-            c = self.at + 2
+        def wait_sides(self):
             self.side_e.wait_recv()
             self.side_w.wait_recv()
+
+        def wait_corners(self):
+            c = self.at + 2
 
             @pl.when(gy > 0)
             def _():
@@ -275,16 +277,23 @@
             low, spin(from_e, -strip * q), spin(from_w, -strip * (q + 1))
         )
 
-    def settle(fields, slot, mask):
-        for r in range(PAD, north + HALO, 8):
+    def mask_rows(slot, mask, lo, hi):
+        for r in range(lo, hi, 8):
             F[0, mask, pl.ds(r, 8), :] = IM[slot, pl.ds(r, 8), :].astype(jnp.float32)
 
+    def settle_sides(fields):
         for f in fields:
             for g, members in enumerate(groups):
                 from_w = RB[0, f, pl.ds(8 * g, 8), :]
                 from_e = RB[1, f, pl.ds(8 * g, 8), :]
                 for q, c in enumerate(members):
                     unpack(f, mid + 8 * c, q, from_w, from_e)
+
+    def settle(fields, slot, mask):
+        mask_rows(slot, mask, PAD, mid)
+        mask_rows(slot, mask, north, north + HALO)
+
+        for f in fields:
             for q in range(HALO // 8):
                 unpack(f, PAD + 8 * q, q, RC[SW, f], RC[SE, f])
                 unpack(f, north + 8 * q, q, RC[NW, f], RC[NE, f])
@@ -313,18 +322,14 @@
                     for q in range(n):
                         F[col, f, pl.ds(north + 8 * (n - 1 - q), 8), :] = sign * block[q]
 
-    early_edges.wait_recv()
-    wait_rows(0, late)
-    settle(range(NCRIT), 0, LAND)
-
     def load(col, f, r):
         return F[col, f, pl.ds(r, 8), :]
 
     def save(col, f, r, value):
         F[col, f, pl.ds(r, 8), :] = value
 
-    for r in range(PAD, north + HALO, 8):
-        for col in range(2):
+    def prepare(lo, hi, col):
+        for r in range(lo, hi, 8):
             m = load(col, MASS, r)
             scaled = load(col, LAND, r) / (m + 0.5)
             save(col, A, r, scaled * m)
@@ -339,6 +344,19 @@
             save(col, G, r, 2.0 * (s1 + s2))
             save(col, M, r, 2.0 * (s1 - s2))
             save(col, T, r, 2.0 * load(col, T, r))
+
+    mask_rows(0, LAND, mid, north)
+    mask_rows(1, REGION, mid, north)
+    prepare(mid, north, 0)
+    early_edges.wait_sides()
+    settle_sides(range(NCRIT))
+    prepare(mid, north, 1)
+    early_edges.wait_corners()
+    wait_rows(0, late)
+    settle(range(NCRIT), 0, LAND)
+    for col in range(2):
+        prepare(PAD, mid, col)
+        prepare(north, north + HALO, col)
 
     def xdiff(f, r):
         c, e = load(0, f, r), load(1, f, r)
@@ -395,8 +413,10 @@
     run(0, HALF, lambda k: forward(k, PAD, north + HALO))
     run(HALF, HALF, lambda k: forward(k, PAD + quarter_halo, north + HALO - quarter_halo))
 
-    late_edges.wait_recv()
+    late_edges.wait_sides()
+    late_edges.wait_corners()
     wait_rows(late, n_plan)
+    settle_sides(range(NCRIT, NF))
     settle(range(NCRIT, NF), 1, REGION)
 
     for r in range(sv_lo, sv_hi, 8):
@@ -606,7 +626,7 @@
             in_specs=[vm],
             out_specs=(hbm, hbm),
             scratch_shapes=[pltpu.SemaphoreType.DMA((2,))],
-        )(both)
+        )(pltpu.with_memory_space_constraint(both, pltpu.VMEM))
 
     block = P(None, "gy", "gx")
     flat = P("gy", "gx")

time: 33.8 us -> 32.1 us (0.950)
  Pallas kernels: 31.6 us -> 30.7 us
  local copies, waits for them, and re-layouts: 0.7 us -> 0 us
    pallas_call x1, Pallas kernels: 1.68 us -> 0.72 us  [per_device(): pl.pallas_call(split_kernel, out_shape=(jax.ShapeDtypeStruct((5, rows, la...]
    unnamed x2 -> x0, local copies, waits for them, and re-layouts: 0.7 us -> none
where the time goes in v3:
time: 32.1 us; the launch traced here: 32 us
  Pallas kernels  30.7 us (96%)
  between operations  1.29 us (4%)
    pallas_call x1, Pallas kernels, per_device(): pl.pallas_call(functools.partial(kernel, nx, ny, rows), out_shape=jax.Sha...  30 us
    pallas_call x1, Pallas kernels, per_device(): pl.pallas_call(split_kernel, out_shape=(jax.ShapeDtypeStruct((5, rows, la...  0.72 us

profile of v3, /device:TPU:0, one launch (start us, length us, event | category | flops | bytes accessed | tf_op | source)
XLA Modules:
  0.0 32.0 jit_solution(3761470722188670173)
XLA Ops:
  1.3 30.0 %shard_map.104.both = f32[7,80,128]{2,1,0:T(8,128)S(1)} custom-call(s32[1]{0:T(128)S(6)} %copy.11.start_ref, f32[2,80,128]{2,1,0:T(8,128)} %vel.1, f32[3,80,128]{2,1,0:T(8,128)} %sts.1, f32[2,80,128]{2,1,0:T(8,128)} %wind.1, f32[80,128]{1,0:T(8,128)} %strength.1, f32[80,128]{1,0:T(8,128)} %mass.1, s32[80,128]{1,0:T(8,128)} %land.1, s32[80,128]{1,0:T(8,128)} %region.1, ...), custom_call_target="tpu_custom_call" | custom-call | tf_op jit(solution)/shard_map/pallas_call | solution.py:593
  31.2 0.7 %shard_map.105 = (f32[5,80,128]{2,1,0:T(8,128)}, f32[2,80,128]{2,1,0:T(8,128)}) custom-call(f32[7,80,128]{2,1,0:T(8,128)S(1)} %shard_map.104.both), custom_call_target="tpu_custom_call" | custom-call | tf_op jit(solution)/shard_map/pallas_call | solution.py:620
